TPU v7x, 128 devices: a whole 4x4x4 slice. The times are simulated.
128 devices in a mesh: prow: 8 (over z_hi, y), pcol: 16 (over x, z_lo, core).
Axes of the slice: x: 4, y: 4, z: 4 (z_hi: 2, z_lo: 2; z = z_hi * 2 + z_lo), core: 2. Of those that a mesh axis runs over, the one named last changes fastest.
Arguments:
- panel_t: float32 [16, 256, 8192], P('pcol', None, 'prow'), may hold values from -0.0625 to 0.0625
- ancestor: float32 [8192, 8192], P('prow', 'pcol'), as said below
- structure: int32 [16, 32], replicated, may hold values 0 or 1
- diag_inv: float32 [16, 256, 256], P('pcol'), may hold values from -6 to 6
Outputs:
- inverse_panel: float32 [4096, 8192], P('pcol', 'prow')
- inverse_diag: float32 [16, 256, 256], P('pcol')
Inputs may be any that keep to these rules, and one draw needn't show every extreme that they name: ancestor is symmetric up to rounding.
All inputs are finite; a program needn't handle non-finite values.
Results may differ from a plain program's by a relative error of at most 0.00007.
Values sent between devices are 32-bit elements; how exact they have to be, the bound alone decides.
A program may use at most 128 MiB of HBM per device.

v0:
```python
import jax
import jax.numpy as jnp
from jax import lax
from jax.sharding import PartitionSpec as P


def copy_for_each(array, axis):
    length = lax.axis_size(axis)
    return lax.all_to_all(
        jnp.broadcast_to(array[None], (length, *array.shape)), axis, 0, 0, tiled=True
    )


def of_everyone(array, axis):
    everything = copy_for_each(array, axis)
    return jnp.sum(everything, axis=0)


def local(panel_t, ancestor, structure, diag_inv):
    local_sn = panel_t.shape[0]
    width = panel_t.shape[1]
    row_span = panel_t.shape[2]
    row_blocks = row_span // width
    col_index = lax.axis_index("pcol")
    row_index = lax.axis_index("prow")
    mine = lax.dynamic_slice(
        structure, (col_index * local_sn, row_index * row_blocks), (local_sn, row_blocks)
    )
    masked = (
        panel_t.reshape(local_sn, width, row_blocks, width)
        * mine.astype(jnp.float32)[:, None, :, None]
    )
    masked = masked.reshape(local_sn, width, row_span)
    prow_size = lax.axis_size("prow")
    rows_here = width // prow_size
    arranged = masked.reshape(local_sn, prow_size, rows_here, row_span).transpose(1, 0, 2, 3)
    gathered = lax.all_gather(arranged, "pcol", axis=1, tiled=True)
    total_nodes = gathered.shape[1]
    flat_rows = gathered.reshape(prow_size * total_nodes * rows_here, row_span)
    reduced = lax.psum_scatter(
        jnp.dot(
            flat_rows, ancestor, precision=lax.Precision.HIGHEST, preferred_element_type=jnp.float32
        ),
        "prow",
        scatter_dimension=0,
        tiled=True,
    )
    moved = lax.all_to_all(
        lax.all_to_all(reduced, "pcol", split_axis=0, concat_axis=1, tiled=True),
        "prow",
        split_axis=1,
        concat_axis=0,
        tiled=True,
    )
    summed = moved.reshape(prow_size, local_sn, rows_here, row_span).transpose(1, 0, 2, 3)
    summed = summed.reshape(local_sn * width, row_span)
    inverse_panel = -summed
    blocks = inverse_panel.reshape(local_sn, width, row_span)
    partial_diag = jnp.einsum("kbj,kcj->kbc", blocks, masked, precision=lax.Precision.HIGHEST)
    inverse_diag = diag_inv - of_everyone(partial_diag, "prow")
    return (inverse_panel, inverse_diag)


def solution(mesh):
    return jax.shard_map(
        local,
        mesh=mesh,
        in_specs=(P("pcol", None, "prow"), P("prow", "pcol"), P(), P("pcol", None, None)),
        out_specs=(P("pcol", "prow"), P("pcol", None, None)),
        check_vma=False,
    )
```

profile of v0, /device:TPU:32, one launch (start us, length us, event | category | flops | bytes accessed | tf_op | source)
XLA Modules:
  0.0 340.1 jit_solution(9076834743426126464)
XLA Ops:
  7.2 0.0 copy-start
  7.2 0.0 all-gather.2.cloned.1.call-start
  7.2 0.9 convert_bitcast_fusion
  8.1 0.1 broadcast_bitcast_fusion
  8.2 2.3 broadcast_multiply_fusion
  10.6 0.0 all-gather.2.cloned.1.call-update
  10.6 0.0 reduce-scatter.2.cloned.1.call-start
  10.6 93.6 %all-gather.2.cloned.1.call-done = f32[8,16,32,1024]{3,2,1,0:T(8,128)} async-done(((f32[8,1,32,1024]{3,2,1,0:T(8,128)}), f32[8,16,32,1024]{3,2,1,0:T(8,128)}) %all-gather.2.cloned.1.call-update) | async-done | bytes 16777232 | tf_op jit(solution)/shard_map/all_gather | solution.py:37
  104.3 0.0 copy-done
  104.3 30.3 %fusion.4 = f32[4096,512]{1,0:T(8,128)} fusion(f32[4096,1024]{1,0:T(8,128)} %bitcast.27, f32[1024,512]{1,0:T(8,128)S(1)} %copy-done), kind=kOutput, calls=%fused_computation.8 | convolution fusion | flops 25769803776 | bytes 27262976 | tf_op jit(solution)/shard_map/dot_general | solution.py:41
  134.5 0.0 reduce-scatter.2.cloned.1.call-update
  134.6 0.0 copy-start.1
  134.6 114.6 %reduce-scatter.2.cloned.1.call-done = f32[512,512]{1,0:T(8,128)} async-done(((f32[4096,512]{1,0:T(8,128)}), f32[512,512]{1,0:T(8,128)}) %reduce-scatter.2.cloned.1.call-update) | async-done | bytes 1048592 | tf_op jit(solution)/shard_map/reduce_scatter | solution.py:40
  249.1 20.5 %all_to_all.34 = f32[16,32,512]{2,1,0:T(8,128)S(1)} all-to-all(f32[16,32,512]{2,1,0:T(8,128)} %bitcast.24), channel_id=1, replica_groups=mesh['prow'=8,'pcol'=16] {'pcol'}, dimensions={0} | all-to-all | bytes 2097152 | tf_op jit(solution)/shard_map/all_to_all | solution.py:49
  269.7 1.6 copy.11
  271.2 2.5 all_to_all.28
  273.8 0.0 copy-start.3
  273.8 1.9 copy.12
  275.6 21.0 %all_to_all.35 = f32[32,8,1024]{2,0,1:T(8,128)S(1)} all-to-all(f32[32,8,1024]{2,0,1:T(8,128)S(1)} %copy.12), channel_id=1, replica_groups=mesh['prow'=8,'pcol'=16] {'prow'}, dimensions={1} | all-to-all | bytes 2097152 | tf_op jit(solution)/shard_map/all_to_all | solution.py:48
  296.7 0.1 neg.13
  296.8 0.0 copy-start.2
  296.8 1.0 copy-done.2
  297.8 0.0 copy-done.1
  297.8 1.0 fusion
  298.8 0.2 broadcast_in_dim.2
  299.0 31.7 %all_to_all.36 = f32[8,1,256,256]{3,2,1,0:T(8,128)} all-to-all(f32[8,1,256,256]{3,2,1,0:T(8,128)S(1)} %broadcast_in_dim.2), channel_id=1, replica_groups=mesh['prow'=8,'pcol'=16] {'prow'}, dimensions={0} | all-to-all | bytes 4194304 | tf_op jit(solution)/shard_map/all_to_all | solution.py:9
  330.8 1.8 reduce_sum.11
  332.5 0.0 copy-done.3
  332.5 0.7 bitcast_subtract_fusion
  (1 shorter events, 0.0 us)
Async XLA Ops:
  7.2 97.1 %copy-start = (f32[1024,512]{1,0:T(8,128)S(1)}, f32[1024,512]{1,0:T(8,128)}, u32[]{:S(2)}) copy-start(f32[1024,512]{1,0:T(8,128)} %param.5) | copy-start | bytes 6291460
  7.2 97.1 %all-gather.2.cloned.1.call-start = ((), (), s32[]{:S(2)}) async-start(), calls=%async_computation.4 | async-start | bytes 17825792 | tf_op jit(solution)/shard_map/all_gather | solution.py:37
  10.6 238.6 %reduce-scatter.2.cloned.1.call-start = ((), (), s32[]{:S(2)}) async-start(), calls=%async_computation.5 | async-start | bytes 9437184 | tf_op jit(solution)/shard_map/reduce_scatter | solution.py:40
  134.6 163.2 %copy-start.1 = (f32[1,256,1024]{2,1,0:T(8,128)S(1)}, f32[1,256,1024]{2,1,0:T(8,128)}, u32[]{:S(2)}) copy-start(f32[1,256,1024]{2,1,0:T(8,128)} %param.4) | copy-start | bytes 3145732
  273.8 58.8 %copy-start.3 = (f32[1,256,256]{2,1,0:T(8,128)S(1)}, f32[1,256,256]{2,1,0:T(8,128)}, u32[]{:S(2)}) copy-start(f32[1,256,256]{2,1,0:T(8,128)} %param.7) | copy-start | bytes 786436
  296.8 1.0 copy-start.2
Sparse Core Ops, SparseCore 0:
  10.7 93.5 all-gather.1
  134.7 114.4 reduce-scatter.1
where the time goes:
time: 340 us
  waiting for transfers between devices  208 us (61%)
  blocking collectives  73.3 us (22%)
  matrix products  31.3 us (9%)
  between operations  14.1 us (4%)
  local copies, waits for them, and re-layouts  7.22 us (2%)
  other arithmetic  5.85 us (2%)
    reduce_scatter x1, waiting for transfers between devices, local(): lax.psum_scatter(jnp.dot(flat_rows, ancestor, precision=lax.Precision.HIG...  115 us
    all_gather x1, waiting for transfers between devices, local(): gathered = lax.all_gather(arranged, 'pcol', axis=1, tiled=True)  93.6 us
    all_to_all x1, blocking collectives, copy_for_each(): lax.all_to_all(jnp.broadcast_to(array[None], (length, *array.shape)), axi...  31.7 us
    dot_general x1, matrix products, local(): jnp.dot(flat_rows, ancestor, precision=lax.Precision.HIGHEST, preferred_e...  30.3 us
    all_to_all x1, blocking collectives, local(): lax.all_to_all(lax.all_to_all(reduced, 'pcol', split_axis=0, concat_axis=...  21 us
    all_to_all x1, blocking collectives, local(): lax.all_to_all(reduced, 'pcol', split_axis=0, concat_axis=1, tiled=True)  20.5 us
  transfers between devices with their start and end apart: 2, of which 2 were waited for; matrix products, arithmetic and copies ran while one was open for 0% of the time, Pallas kernels for 0%

commit v1 on v0

v1 whole, which is shorter than its diff:
```python
import functools

import jax
import jax.numpy as jnp
from jax import lax
from jax.experimental import pallas as pl
from jax.experimental.pallas import tpu as pltpu
from jax.sharding import PartitionSpec as P

MESH = pl.DeviceIdType.MESH
F32 = jnp.float32
BF16 = jnp.bfloat16

DX = (0, 0, -1, 1, 0, -1, 1, 0, 2, 2, -1, 1, 2, -1, 1, 2)
DZ = (0, 0, 0, 0, 1, 0, 0, 1, 0, 0, 1, 1, 1, 1, 1, 1)
TO_RIGHT = {0: 2, 1: 5, 2: 8, 4: 10, 7: 13}
TO_LEFT = {1: 3, 0: 6, 3: 9, 7: 11, 4: 14}
TO_Z = {0: 4, 1: 7, 8: 12, 9: 15}
EVENTS = 16
NX, NY, NZ = 4, 4, 2


def split(value):
    high = value.astype(BF16)
    low = (value - high.astype(F32)).astype(BF16)
    return high, low


def kernel(
    panel, ancestor, structure, diag_inv, panel_out, diag_out,
    gathered, b_high, b_low, a_high, a_low, partial, got1, got2, owned, got3, final, arrived, own_diag, got_diag, sum_diag,
    all_diag,
    gather_send, gather_recv, core_send, core_recv, send1, recv1, send2, recv2, send3, recv3, send4, recv4, send5, recv5,
    send6, recv6,
):
    row = lax.axis_index("prow")
    col = lax.axis_index("pcol")
    core = lax.rem(col, 2)
    zl = lax.rem(col // 2, 2)
    x = col // 4
    y = lax.rem(row, NY)
    zh = row // NY

    def at_col(xx, zz, cc):
        return (xx * 2 + zz) * 2 + cc

    right = (row, at_col(lax.rem(x + 1, NX), zl, core))
    left = (row, at_col(lax.rem(x + NX - 1, NX), zl, core))
    z_pair = (row, at_col(x, 1 - zl, core))
    twin = (row, at_col(x, zl, 1 - core))
    y_up, y_down, y_far = lax.rem(y + 1, NY), lax.rem(y + NY - 1, NY), lax.rem(y + 2, NY)
    up = (zh * NY + y_up, col)
    down = (zh * NY + y_down, col)
    z_far = ((1 - zh) * NY + y, col)
    home_row = col // 2
    mine_home = (home_row == row).astype(jnp.int32)

    barrier = pltpu.get_barrier_semaphore()

    def greet(device):
        pl.semaphore_signal(barrier, inc=1, device_id=device, device_id_type=MESH)

    for device in (right, left, z_pair, twin):
        greet(device)
    for step in range(1, 8):
        greet((lax.rem(row + step, 8), col))
    for other in range(8):
        for half in range(2):
            source = (other, 2 * row + half)

            @pl.when(jnp.logical_or(other != row, 2 * row + half != col))
            def _():
                greet(source)

    for n in range(2):
        high, low = split(ancestor[:, n * 256 : (n + 1) * 256])
        b_high[n] = high
        b_low[n] = low

    def load(unit, event, value):
        xx = lax.rem(x + NX + DX[event], NX)
        zz = zl if DZ[event] == 0 else 1 - zl
        cc = core if unit == 0 else 1 - core
        node = at_col(xx, zz, cc)
        for block in range(4):
            mask = structure[node, row * 4 + block].astype(F32)
            high, low = split(value[:, block * 256 : (block + 1) * 256] * mask)
            a_high[unit * 128 : (unit + 1) * 128, block * 256 : (block + 1) * 256] = high
            a_low[unit * 128 : (unit + 1) * 128, block * 256 : (block + 1) * 256] = low

    pl.semaphore_wait(barrier, 27 - mine_home)

    waits = []

    def send(source, target, send_sem, recv_sem, device):
        copy = pltpu.make_async_remote_copy(
            src_ref=source, dst_ref=target, send_sem=send_sem, recv_sem=recv_sem, device_id=device, device_id_type=MESH
        )
        copy.start()
        waits.append(copy)
        return copy

    def mine(event):
        if event < 2:
            return panel.at[0, pl.ds(event * 128, 128), :]
        return gathered.at[0, event]

    def wait_recv(target, send_sem, recv_sem):
        pltpu.make_async_remote_copy(
            src_ref=target, dst_ref=target, send_sem=send_sem, recv_sem=recv_sem, device_id=twin, device_id_type=MESH
        ).wait_recv()

    count = [0]

    def arrive(event):
        if event >= 2:
            wait_recv(gathered.at[0, event], gather_send.at[0], gather_recv.at[event])
        for table, device in ((TO_RIGHT, right), (TO_LEFT, left), (TO_Z, z_pair)):
            if event in table:
                there = table[event]
                send(mine(event), gathered.at[0, there], gather_send.at[count[0]], gather_recv.at[there], device)
                count[0] += 1
        send(mine(event), gathered.at[1, event], core_send.at[event], core_recv.at[event], twin)

    def multiply(event):
        load(0, event, mine(event))
        wait_recv(gathered.at[1, event], core_send.at[0], core_recv.at[event])
        load(1, event, gathered.at[1, event])

        @pl.loop(0, 2)
        def _(n):
            high = a_high[...]
            product = (
                jnp.dot(high, b_high[n], preferred_element_type=F32)
                + jnp.dot(high, b_low[n], preferred_element_type=F32)
                + jnp.dot(a_low[...], b_high[n], preferred_element_type=F32)
            )
            for unit in range(2):
                for yy in range(NY):
                    partial[event, yy, n, unit * 32 : (unit + 1) * 32, :] = product[unit * 128 + yy * 32 : unit * 128 + yy * 32 + 32, :]

        send(partial.at[event, y_far, 0], got1.at[event, 0], send1.at[event, 0], recv1.at[event, 0], up)
        send(partial.at[event, y_far, 1], got1.at[event, 1], send1.at[event, 1], recv1.at[event, 1], down)

    def stage2(event):
        for way, (yy, device) in enumerate(((y_up, up), (y_down, down))):
            wait_recv(got1.at[event, way], send1.at[event, way], recv1.at[event, way])
            partial[event, yy, way] += got1[event, way]
            send(partial.at[event, yy], got2.at[event, way], send2.at[event, way], recv2.at[event, way], device)

    def stage3(event):
        for way in range(2):
            wait_recv(got2.at[event, way], send2.at[event, way], recv2.at[event, way])
        for n in range(2):
            total = partial[event, y, n] + got2[event, 0, n] + got2[event, 1, n]
            for unit in range(2):
                for hz in range(2):
                    start = unit * 32 + hz * 16
                    owned[event, hz, unit, :, n * 256 : (n + 1) * 256] = total[start : start + 16, :]
        send(owned.at[event, 1 - zh], got3.at[event], send3.at[event], recv3.at[event], z_far)

    def home(event, unit):
        xx = lax.rem(x + NX + DX[event], NX)
        zz = zl if DZ[event] == 0 else 1 - zl
        cc = core if unit == 0 else 1 - core
        return at_col(xx, zz, cc)

    def stage4(event):
        wait_recv(got3.at[event], send3.at[event], recv3.at[event])
        final[event] = owned[event, zh] + got3[event]
        half = event % 2
        start = pl.multiple_of(half * 128 + y * 32 + zh * 16, 16)
        for unit in range(2):
            node = home(event, unit)
            here = jnp.logical_and(home_row == row, node == col)
            target = arrived.at[core, pl.ds(start, 16), :]

            @pl.when(here)
            def _():
                arrived[core, pl.ds(start, 16), :] = final[event, unit]

            @pl.when(jnp.logical_not(here))
            def _():
                pltpu.make_async_remote_copy(
                    src_ref=final.at[event, unit], dst_ref=target, send_sem=send4.at[event, unit],
                    recv_sem=recv4.at[core, half, row], device_id=(home_row, node), device_id_type=MESH,
                ).start()

    for step in range(EVENTS + 3):
        if step < EVENTS:
            arrive(step)
            multiply(step)
        if 0 <= step - 1 < EVENTS:
            stage2(step - 1)
        if 0 <= step - 2 < EVENTS:
            stage3(step - 2)
        if 0 <= step - 3 < EVENTS:
            stage4(step - 3)

    for side in range(2):
        for half in range(2):
            for source in range(8):
                start = half * 128 + (source % 4) * 32 + (source // 4) * 16
                there = jnp.logical_and(source == row, 2 * row + side == col)

                @pl.when(jnp.logical_not(there))
                def _():
                    wait_recv(arrived.at[side, start : start + 16, :], send4.at[0, 0], recv4.at[side, half, source])

    for block in range(4):
        mask = structure[col, row * 4 + block].astype(F32)
        high, low = split(panel[0, :, block * 256 : (block + 1) * 256] * mask)
        a_high[:, block * 256 : (block + 1) * 256] = high
        a_low[:, block * 256 : (block + 1) * 256] = low
    contract = functools.partial(
        lax.dot_general, dimension_numbers=(((1,), (1,)), ((), ())), preferred_element_type=F32
    )
    total = jnp.zeros((256, 256), F32)
    for side in range(2):
        value = -arrived[side]
        panel_out[:, side * 512 : (side + 1) * 512] = value
        high, low = split(value)
        right_high = a_high[:, side * 512 : (side + 1) * 512]
        right_low = a_low[:, side * 512 : (side + 1) * 512]
        total = total + contract(high, right_high) + contract(high, right_low) + contract(low, right_high)
    own_diag[...] = total
    for step in range(1, 8):
        other = lax.rem(row + step, 8)
        piece = pl.ds(pl.multiple_of(other * 32, 32), 32)
        send(own_diag.at[piece, :], got_diag.at[row], send5.at[step], recv5.at[row], (other, col))
    here = pl.ds(pl.multiple_of(row * 32, 32), 32)
    result = diag_inv[0, here, :] - own_diag[here, :]
    for step in range(1, 8):
        other = lax.rem(row + step, 8)
        wait_recv(got_diag.at[other], send5.at[step], recv5.at[other])
        result = result - got_diag[other]
    sum_diag[...] = result
    for step in range(1, 8):
        other = lax.rem(row + step, 8)
        send(sum_diag, all_diag.at[row], send6.at[step], recv6.at[row], (other, col))
    diag_out[0, here, :] = result
    for step in range(1, 8):
        other = lax.rem(row + step, 8)
        wait_recv(all_diag.at[other], send6.at[step], recv6.at[other])
        diag_out[0, pl.ds(pl.multiple_of(other * 32, 32), 32), :] = all_diag[other]

    for copy in waits:
        copy.wait_send()
    for event in range(EVENTS):
        for unit in range(2):
            node = home(event, unit)

            @pl.when(jnp.logical_or(home_row != row, node != col))
            def _():
                pltpu.make_async_remote_copy(
                    src_ref=final.at[event, unit], dst_ref=final.at[event, unit], send_sem=send4.at[event, unit],
                    recv_sem=recv4.at[0, 0, 0], device_id=twin, device_id_type=MESH,
                ).wait_send()


def local(panel_t, ancestor, structure, diag_inv):
    vmem = pltpu.VMEM
    dma = pltpu.SemaphoreType.DMA
    return pl.pallas_call(
        kernel,
        out_shape=(
            jax.ShapeDtypeStruct((256, 1024), F32),
            jax.ShapeDtypeStruct((1, 256, 256), F32),
        ),
        in_specs=[
            pl.BlockSpec(memory_space=vmem),
            pl.BlockSpec(memory_space=vmem),
            pl.BlockSpec(memory_space=pltpu.SMEM),
            pl.BlockSpec(memory_space=vmem),
        ],
        out_specs=(pl.BlockSpec(memory_space=vmem), pl.BlockSpec(memory_space=vmem)),
        scratch_shapes=[
            vmem((2, EVENTS, 128, 1024), F32),
            vmem((2, 1024, 256), BF16),
            vmem((2, 1024, 256), BF16),
            vmem((256, 1024), BF16),
            vmem((256, 1024), BF16),
            vmem((EVENTS, NY, 2, 64, 256), F32),
            vmem((EVENTS, 2, 64, 256), F32),
            vmem((EVENTS, 2, 2, 64, 256), F32),
            vmem((EVENTS, 2, 2, 16, 512), F32),
            vmem((EVENTS, 2, 16, 512), F32),
            vmem((EVENTS, 2, 16, 512), F32),
            vmem((2, 256, 512), F32),
            vmem((256, 256), F32),
            vmem((8, 32, 256), F32),
            vmem((32, 256), F32),
            vmem((8, 32, 256), F32),
            dma((14,)),
            dma((EVENTS,)),
            dma((EVENTS,)),
            dma((EVENTS,)),
            dma((EVENTS, 2)),
            dma((EVENTS, 2)),
            dma((EVENTS, 2)),
            dma((EVENTS, 2)),
            dma((EVENTS,)),
            dma((EVENTS,)),
            dma((EVENTS, 2)),
            dma((2, 2, 8)),
            dma((8,)),
            dma((8,)),
            dma((8,)),
            dma((8,)),
        ],
        compiler_params=pltpu.CompilerParams(
            collective_id=0, has_side_effects=True, vmem_limit_bytes=60 * 1024 * 1024
        ),
        name="level_update",
    )(panel_t, ancestor, structure, diag_inv)


def solution(mesh):
    return jax.shard_map(
        local,
        mesh=mesh,
        in_specs=(P("pcol", None, "prow"), P("prow", "pcol"), P(), P("pcol", None, None)),
        out_specs=(P("pcol", "prow"), P("pcol", None, None)),
        check_vma=False,
    )
```

time: 340 us -> 175 us (0.51)
  waiting for transfers between devices: 208 us -> 0 us
  Pallas kernels: 0 us -> 169 us
  blocking collectives: 73.3 us -> 0 us
  matrix products: 31.3 us -> 0 us
  between operations: 14.1 us -> 0.65 us
  other arithmetic: 5.85 us -> 0 us
  local copies, waits for them, and re-layouts: 7.22 us -> 3.06 us
    pallas_call x0 -> x1, Pallas kernels: none -> 169 us  [local(): pl.pallas_call(kernel, out_shape=(jax.ShapeDtypeStruct((256, 1024), F32),...]
    reduce_scatter x1 -> x0, waiting for transfers between devices: 115 us -> none  [local(): lax.psum_scatter(jnp.dot(flat_rows, ancestor, precision=lax.Precision.HIG...]
    all_gather x1 -> x0, waiting for transfers between devices: 93.6 us -> none  [local(): gathered = lax.all_gather(arranged, 'pcol', axis=1, tiled=True)]
    all_to_all x3 -> x0, blocking collectives: 73.3 us -> none  [the longest x1 31.7 us: copy_for_each(): lax.all_to_all(jnp.broadcast_to(array[None], (length, *array.shape)), axi...]
    dot_general x2 -> x0, matrix products: 31.3 us -> none  [the longest x1 30.3 us: local(): jnp.dot(flat_rows, ancestor, precision=lax.Precision.HIGHEST, preferred_e...]
    all_to_all x3 -> x0, local copies, waits for them, and re-layouts: 5.99 us -> none  [the longest x2 4.4 us: local(): lax.all_to_all(lax.all_to_all(reduced, 'pcol', split_axis=0, concat_axis=...]
  transfers between devices with their start and end apart: 2 -> 0, of which waited for: 2 -> 0; matrix products, arithmetic and copies ran while one was open for 0% -> 0% of each run, Pallas kernels for 0% -> 0%
where the time goes in v1:
time: 175 us; the launch traced here: 173 us
  Pallas kernels  169 us (97%)
  local copies, waits for them, and re-layouts  3.06 us (2%)
    pallas_call x1, Pallas kernels, local(): pl.pallas_call(kernel, out_shape=(jax.ShapeDtypeStruct((256, 1024), F32),...  169 us

profile of v1, /device:TPU:32, one launch (start us, length us, event | category | flops | bytes accessed | tf_op | source)
XLA Modules:
  0.0 173.2 jit_solution(9781989005938739355)
XLA Ops:
  0.6 169.5 %level_update.1 = (f32[256,1024]{1,0:T(8,128)}, f32[1,256,256]{2,1,0:T(8,128)}) custom-call(f32[1,256,1024]{2,1,0:T(8,128)} %panel.1, f32[1024,512]{1,0:T(8,128)} %ancestor.1, s32[16,32]{1,0:T(8,128)} %structure.1, f32[1,256,256]{2,1,0:T(8,128)} %diag_inv.1), custom_call_target="tpu_custom_call" | custom-call | tf_op jit(solution)/shard_map/level_update/pallas_call | solution.py:264
  170.1 0.0 copy-start
  170.1 2.3 %copy.8 = f32[256,1024]{1,0:T(8,128)} copy(f32[256,1024]{1,0:T(8,128)} %get-tuple-element.4) | data formatting | bytes 2097152
  172.5 0.0 copy-done
  172.5 0.7 copy.9
Async XLA Ops:
  170.1 2.4 %copy-start = (f32[1,256,256]{2,1,0:T(8,128)S(1)}, f32[1,256,256]{2,1,0:T(8,128)}, u32[]{:S(2)}) copy-start(f32[1,256,256]{2,1,0:T(8,128)} %get-tuple-element.5) | copy-start | bytes 786436

commit v2 on v1

v2 whole, which is shorter than its diff:
```python
import functools

import jax
import jax.numpy as jnp
from jax import lax
from jax.experimental import pallas as pl
from jax.experimental.pallas import tpu as pltpu
from jax.sharding import PartitionSpec as P

MESH = pl.DeviceIdType.MESH
F32 = jnp.float32
BF16 = jnp.bfloat16

DX = (0, 0, -1, 1, 1, -1, 2, 2)
EVENTS = 8
TO_RIGHT = {0: 2, 1: 5, 2: 6}
TO_LEFT = {1: 3, 0: 4, 3: 7}
PAIRS = ((0, 1), (2, 5), (4, 3), (6, 7))
ITEMS = 16
ORDER = (
    "M0 M1 A0 B0", "A1 B1 C0 F2", "F3 M2 M3 C1", "A2 B2 A3 B3", "F5 F4 G2 M8", "C2 M5 M4 M9",
    "M10 A5 A8 B5", "B8 A4 B4 C3", "A9 F6 F7 B9", "A10 B10 M6 M7", "M11 C5 C8 C4", "G3 M12 M13 M14",
    "M15 A6 B6 D0", "A7 B7 D1 D2", "D3 D5 C9 A11", "B11 C10 D8 A12", "B12 D4 A13 B13", "A14 B14 A15 B15",
    "D9 C6 D10 C7", "D6 D7 C11 C12", "D11 C13 D12 C14", "D13 C15 D14 D15",
)
NX, NY = 4, 4
WINDOWS = (8, 4, 4)
PACE = 2


def parts(item):
    if item < EVENTS:
        return ((item, 0), (item, 1))
    first, second = PAIRS[(item - EVENTS) % 4]
    block = 2 + (item - EVENTS) // 4
    return ((first, block), (second, block))


def split(value):
    high = value.astype(BF16)
    low = (value - high.astype(F32)).astype(BF16)
    return high, low


def pick(table, index):
    value = jnp.int32(table[0])
    for place in range(1, len(table)):
        value = jnp.where(index == place, jnp.int32(table[place]), value)
    return value


def kernel(
    panel, ancestor, structure, diag_inv, panel_out, diag_out,
    gathered, b_pair, b_high, b_low, a_high, a_low, partial, got1, got2, owned, got3, final, arrived, own_diag, got_diag,
    sum_diag, all_diag,
    gather_send, gather_recv, core_send, core_recv, pair_send, pair_recv, send1, recv1, send2, recv2, send3, recv3, send4, recv4,
    send5, recv5, send6, recv6,
):
    row = lax.axis_index("prow")
    col = lax.axis_index("pcol")
    core = lax.rem(col, 2)
    zl = lax.rem(col // 2, 2)
    x = col // 4
    y = lax.rem(row, NY)
    zh = row // NY

    def at_col(xx, zz, cc):
        return (xx * 2 + zz) * 2 + cc

    right = (row, at_col(lax.rem(x + 1, NX), zl, core))
    left = (row, at_col(lax.rem(x + NX - 1, NX), zl, core))
    z_pair = (row, at_col(x, 1 - zl, core))
    twin = (row, at_col(x, zl, 1 - core))
    y_up, y_down, y_far = lax.rem(y + 1, NY), lax.rem(y + NY - 1, NY), lax.rem(y + 2, NY)
    up = (zh * NY + y_up, col)
    down = (zh * NY + y_down, col)
    z_far = ((1 - zh) * NY + y, col)
    home_rows = (x * 2 + zl, x * 2 + 1 - zl)
    mine_home = (row // 2 == x).astype(jnp.int32)

    barrier = pltpu.get_barrier_semaphore()

    def greet(device):
        pl.semaphore_signal(barrier, inc=1, device_id=device, device_id_type=MESH)

    for device in (right, left, z_pair, twin):
        greet(device)
    for step in range(1, 8):
        greet((lax.rem(row + step, 8), col))
    for other in range(8):
        for side in range(2):
            source = at_col(row // 2, zl, side)

            @pl.when(jnp.logical_or(other != row, source != col))
            def _():
                greet((other, source))

    def take_columns(block, value):
        high, low = split(value)
        b_high[block] = high
        b_low[block] = low

    for block in range(2):
        take_columns(block, ancestor[:, block * 256 : (block + 1) * 256])

    pl.semaphore_wait(barrier, 27 - mine_home)

    waits = []

    def send(source, target, send_sem, recv_sem, device):
        copy = pltpu.make_async_remote_copy(
            src_ref=source, dst_ref=target, send_sem=send_sem, recv_sem=recv_sem, device_id=device, device_id_type=MESH
        )
        copy.start()
        waits.append(copy)

    def wait_recv(target, send_sem, recv_sem):
        pltpu.make_async_remote_copy(
            src_ref=target, dst_ref=target, send_sem=send_sem, recv_sem=recv_sem, device_id=twin, device_id_type=MESH
        ).wait_recv()

    def mine(event):
        if event < 2:
            return panel.at[0, pl.ds(event * 128, 128), :]
        return gathered.at[0, event]

    count = [0]

    def pass_on(event, table, device):
        if event in table:
            there = table[event]
            send(mine(event), gathered.at[0, there], gather_send.at[count[0]], gather_recv.at[there], device)
            count[0] += 1

    def to_twin(event):
        send(mine(event), gathered.at[1, event], core_send.at[event], core_recv.at[event], twin)

    def arrive(event):
        wait_recv(gathered.at[0, event], gather_send.at[0], gather_recv.at[event])
        pass_on(event, TO_RIGHT, right)
        pass_on(event, TO_LEFT, left)
        to_twin(event)

    def take_pair(block):
        wait_recv(b_pair.at[block - 2], pair_send.at[block - 2], pair_recv.at[block - 2])
        take_columns(block, b_pair[block - 2])

    def home_node(dx, unit):
        return at_col(lax.rem(x + NX + dx, NX), zl, core if unit == 0 else 1 - core)

    def load(event, unit, value):
        node = home_node(DX[event], unit)
        for block in range(4):
            mask = structure[node, row * 4 + block].astype(F32)
            high, low = split(value[:, block * 256 : (block + 1) * 256] * mask)
            a_high[event, unit * 128 : (unit + 1) * 128, block * 256 : (block + 1) * 256] = high
            a_low[event, unit * 128 : (unit + 1) * 128, block * 256 : (block + 1) * 256] = low

    def multiply(item):
        if item < EVENTS:
            load(item, 0, mine(item))
            wait_recv(gathered.at[1, item], core_send.at[0], core_recv.at[item])
            load(item, 1, gathered.at[1, item])
        (event0, block0), (event1, block1) = parts(item)

        @pl.loop(0, 2)
        def _(n):
            event = event0 + n * (event1 - event0)
            block = block0 + n * (block1 - block0)
            high = a_high[event]
            product = (
                jnp.dot(high, b_high[block], preferred_element_type=F32)
                + jnp.dot(high, b_low[block], preferred_element_type=F32)
                + jnp.dot(a_low[event], b_high[block], preferred_element_type=F32)
            )
            for unit in range(2):
                for yy in range(NY):
                    start = unit * 128 + yy * 32
                    partial[item, yy, n, unit * 32 : (unit + 1) * 32, :] = product[start : start + 32, :]

        send(partial.at[item, y_far, 0], got1.at[item, 0], send1.at[item, 0], recv1.at[item, 0], up)
        send(partial.at[item, y_far, 1], got1.at[item, 1], send1.at[item, 1], recv1.at[item, 1], down)

    def stage2(item, way):
        yy, device = ((y_up, up), (y_down, down))[way]
        wait_recv(got1.at[item, way], send1.at[item, way], recv1.at[item, way])
        partial[item, yy, way] += got1[item, way]
        send(partial.at[item, yy], got2.at[item, way], send2.at[item, way], recv2.at[item, way], device)

    def stage3(item):
        for way in range(2):
            wait_recv(got2.at[item, way], send2.at[item, way], recv2.at[item, way])
        for n in range(2):
            total = partial[item, y, n] + got2[item, 0, n] + got2[item, 1, n]
            for unit in range(2):
                for hz in range(2):
                    start = unit * 32 + hz * 16
                    owned[item, hz, unit, n] = total[start : start + 16, :]
        send(owned.at[item, 1 - zh], got3.at[item], send3.at[item], recv3.at[item], z_far)

    def stage4(item):
        wait_recv(got3.at[item], send3.at[item], recv3.at[item])
        final[item] = owned[item, zh] + got3[item]

    def send_piece(item, dx, own, place, unit, act):
        node = home_node(dx, unit)
        home_row = home_rows[0] if own else home_rows[1]
        here = jnp.logical_and(home_row == row, node == col)
        start = pl.multiple_of(y * 32 + zh * 16, 16)
        if own:
            target = arrived.at[core, :, place, pl.ds(start, 16), :]
        else:
            target = arrived.at[core, place, :, pl.ds(start, 16), :]
        copy = pltpu.make_async_remote_copy(
            src_ref=final.at[item, unit], dst_ref=target, send_sem=send4.at[item, unit], recv_sem=recv4.at[core, place, row],
            device_id=(home_row, node), device_id_type=MESH,
        )
        if act:

            @pl.when(here)
            def _():
                if own:
                    arrived[core, :, place, pl.ds(start, 16), :] = final[item, unit]
                else:
                    arrived[core, place, :, pl.ds(start, 16), :] = final[item, unit]

        @pl.when(jnp.logical_not(here))
        def _():
            if act:
                copy.start()
            else:
                copy.wait_send()

    ITEM_DX = DX + tuple(DX[parts(item)[0][0]] for item in range(EVENTS, ITEMS))

    def send_home(items, turn):
        item = pick(items, lax.rem(row + turn, len(items)))
        dx = pick(ITEM_DX, item)
        for unit in range(2):

            @pl.when(item < EVENTS)
            def _():
                send_piece(item, dx, True, lax.rem(item, 2), unit, True)

            @pl.when(item >= EVENTS)
            def _():
                send_piece(item, dx, False, (item - EVENTS) // 4, unit, True)

    pass_on(0, TO_RIGHT, right)
    pass_on(1, TO_LEFT, left)
    for block in range(2):
        send(ancestor.at[:, pl.ds(block * 256, 256)], b_pair.at[block], pair_send.at[block], pair_recv.at[block], z_pair)
    to_twin(0)
    to_twin(1)
    pass_on(1, TO_RIGHT, right)
    pass_on(0, TO_LEFT, left)
    work = {
        "F": arrive,
        "G": take_pair,
        "M": multiply,
        "A": lambda item: stage2(item, 0),
        "B": lambda item: stage2(item, 1),
        "C": stage3,
        "D": stage4,
    }
    batch, ready, sizes = [], [], list(WINDOWS)
    for step in " ".join(ORDER).split():
        item = int(step[1:])
        work[step[0]](item)
        if step[0] == "D":
            batch.append(item)
            for _ in range(min(PACE, len(ready))):
                send_home(*ready.pop(0))
            if len(batch) == sizes[0]:
                ready += [(tuple(batch), turn) for turn in range(len(batch))]
                batch = []
                sizes.pop(0)
    for items, turn in ready:
        send_home(items, turn)

    for block in range(4):
        mask = structure[col, row * 4 + block].astype(F32)
        high, low = split(panel[0, :, block * 256 : (block + 1) * 256] * mask)
        a_high[0, :, block * 256 : (block + 1) * 256] = high
        a_low[0, :, block * 256 : (block + 1) * 256] = low

    for side in range(2):
        for place in range(2):
            for source in range(8):
                there = jnp.logical_and(source == row, at_col(row // 2, zl, side) == col)

                @pl.when(jnp.logical_not(there))
                def _():
                    wait_recv(final.at[0, 0], send4.at[0, 0], recv4.at[side, place, source])

    contract = functools.partial(
        lax.dot_general, dimension_numbers=(((1,), (1,)), ((), ())), preferred_element_type=F32
    )
    total = jnp.zeros((256, 256), F32)
    for side in range(2):
        for block in range(2):
            columns = slice(side * 512 + block * 256, side * 512 + block * 256 + 256)
            value = -arrived[side, block].reshape(256, 256)
            panel_out[:, columns] = value
            high, low = split(value)
            right_high = a_high[0, :, columns]
            right_low = a_low[0, :, columns]
            total = total + contract(high, right_high) + contract(high, right_low) + contract(low, right_high)
    own_diag[...] = total
    for step in range(1, 8):
        other = lax.rem(row + step, 8)
        piece = pl.ds(pl.multiple_of(other * 32, 32), 32)
        send(own_diag.at[piece, :], got_diag.at[row], send5.at[step], recv5.at[row], (other, col))
    here = pl.ds(pl.multiple_of(row * 32, 32), 32)
    result = diag_inv[0, here, :] - own_diag[here, :]
    for step in range(1, 8):
        other = lax.rem(row + step, 8)
        wait_recv(got_diag.at[other], send5.at[step], recv5.at[other])
        result = result - got_diag[other]
    sum_diag[...] = result
    for step in range(1, 8):
        other = lax.rem(row + step, 8)
        send(sum_diag, all_diag.at[row], send6.at[step], recv6.at[row], (other, col))
    diag_out[0, here, :] = result
    for step in range(1, 8):
        other = lax.rem(row + step, 8)
        wait_recv(all_diag.at[other], send6.at[step], recv6.at[other])
        diag_out[0, pl.ds(pl.multiple_of(other * 32, 32), 32), :] = all_diag[other]

    for copy in waits:
        copy.wait_send()
    for item in range(ITEMS):
        for unit in range(2):
            own = item < EVENTS
            place = item % 2 if own else (item - EVENTS) // 4
            send_piece(item, ITEM_DX[item], own, place, unit, False)


def local(panel_t, ancestor, structure, diag_inv):
    vmem = pltpu.VMEM
    dma = pltpu.SemaphoreType.DMA
    return pl.pallas_call(
        kernel,
        out_shape=(
            jax.ShapeDtypeStruct((256, 1024), F32),
            jax.ShapeDtypeStruct((1, 256, 256), F32),
        ),
        in_specs=[
            pl.BlockSpec(memory_space=vmem),
            pl.BlockSpec(memory_space=vmem),
            pl.BlockSpec(memory_space=pltpu.SMEM),
            pl.BlockSpec(memory_space=vmem),
        ],
        out_specs=(pl.BlockSpec(memory_space=vmem), pl.BlockSpec(memory_space=vmem)),
        scratch_shapes=[
            vmem((2, EVENTS, 128, 1024), F32),
            vmem((2, 1024, 256), F32),
            vmem((4, 1024, 256), BF16),
            vmem((4, 1024, 256), BF16),
            vmem((EVENTS, 256, 1024), BF16),
            vmem((EVENTS, 256, 1024), BF16),
            vmem((ITEMS, NY, 2, 64, 256), F32),
            vmem((ITEMS, 2, 64, 256), F32),
            vmem((ITEMS, 2, 2, 64, 256), F32),
            vmem((ITEMS, 2, 2, 2, 16, 256), F32),
            vmem((ITEMS, 2, 2, 16, 256), F32),
            vmem((ITEMS, 2, 2, 16, 256), F32),
            vmem((2, 2, 2, 128, 256), F32),
            vmem((256, 256), F32),
            vmem((8, 32, 256), F32),
            vmem((32, 256), F32),
            vmem((8, 32, 256), F32),
            dma((6,)),
            dma((EVENTS,)),
            dma((EVENTS,)),
            dma((EVENTS,)),
            dma((2,)),
            dma((2,)),
            dma((ITEMS, 2)),
            dma((ITEMS, 2)),
            dma((ITEMS, 2)),
            dma((ITEMS, 2)),
            dma((ITEMS,)),
            dma((ITEMS,)),
            dma((ITEMS, 2)),
            dma((2, 2, 8)),
            dma((8,)),
            dma((8,)),
            dma((8,)),
            dma((8,)),
        ],
        compiler_params=pltpu.CompilerParams(
            collective_id=0, has_side_effects=True, vmem_limit_bytes=60 * 1024 * 1024
        ),
        name="level_update",
    )(panel_t, ancestor, structure, diag_inv)


def solution(mesh):
    return jax.shard_map(
        local,
        mesh=mesh,
        in_specs=(P("pcol", None, "prow"), P("prow", "pcol"), P(), P("pcol", None, None)),
        out_specs=(P("pcol", "prow"), P("pcol", None, None)),
        check_vma=False,
    )
```

time: 175 us -> 133 us (0.76)
  Pallas kernels: 169 us -> 129 us
    pallas_call x1, Pallas kernels: 169 us -> 129 us  [local(): pl.pallas_call(kernel, out_shape=(jax.ShapeDtypeStruct((256, 1024), F32),...]
where the time goes in v2:
time: 133 us; the launch traced here: 132 us
  Pallas kernels  129 us (97%)
  local copies, waits for them, and re-layouts  3.06 us (2%)
    pallas_call x1, Pallas kernels, local(): pl.pallas_call(kernel, out_shape=(jax.ShapeDtypeStruct((256, 1024), F32),...  129 us
    unnamed x4, local copies, waits for them, and re-layouts  3.06 us

profile of v2, /device:TPU:32, one launch (start us, length us, event | category | flops | bytes accessed | tf_op | source)
XLA Modules:
  0.0 132.3 jit_solution(4926072156966906816)
XLA Ops:
  0.6 128.6 %level_update.1 = (f32[256,1024]{1,0:T(8,128)}, f32[1,256,256]{2,1,0:T(8,128)}) custom-call(f32[1,256,1024]{2,1,0:T(8,128)} %panel.1, f32[1024,512]{1,0:T(8,128)} %ancestor.1, s32[16,32]{1,0:T(8,128)} %structure.1, f32[1,256,256]{2,1,0:T(8,128)} %diag_inv.1), custom_call_target="tpu_custom_call" | custom-call | tf_op jit(solution)/shard_map/level_update/pallas_call | solution.py:342
  129.2 0.0 copy-start
  129.2 2.3 %copy.8 = f32[256,1024]{1,0:T(8,128)} copy(f32[256,1024]{1,0:T(8,128)} %get-tuple-element.4) | data formatting | bytes 2097152
  131.6 0.0 copy-done
  131.6 0.7 copy.9
Async XLA Ops:
  129.2 2.4 %copy-start = (f32[1,256,256]{2,1,0:T(8,128)S(1)}, f32[1,256,256]{2,1,0:T(8,128)}, u32[]{:S(2)}) copy-start(f32[1,256,256]{2,1,0:T(8,128)} %get-tuple-element.5) | copy-start | bytes 786436

commit v3 on v2

v3 whole, which is shorter than its diff:
```python
import functools

import jax
import jax.numpy as jnp
from jax import lax
from jax.experimental import pallas as pl
from jax.experimental.pallas import tpu as pltpu
from jax.sharding import PartitionSpec as P

MESH = pl.DeviceIdType.MESH
F32 = jnp.float32
BF16 = jnp.bfloat16

DX = (0, 0, 0, 0, -1, -1, 1, 1, -1, -1, 1, 1, 2, 2, 2, 2)
QUARTER = (0, 1, 2, 3, 0, 1, 3, 2, 2, 3, 1, 0, 0, 1, 3, 2)
EVENTS = 16
TO_RIGHT = {0: 4, 1: 5, 2: 8, 3: 9, 4: 12, 5: 13}
TO_LEFT = {3: 6, 2: 7, 1: 10, 0: 11, 6: 14, 7: 15}
PAIRS = ((0, 1), (2, 3), (4, 5), (7, 6), (8, 9), (11, 10), (12, 13), (15, 14))
ITEMS = 32
ORDER = (
    "M0 M1 M2 M3", "A0 B0 A1 B1", "F4 F6 A2 B2", "A3 B3 M4 M6", "C0 C1 F5 F7", "C2 C3 M5 A4",
    "A6 B4 B6 M7", "F8 F10 A5 B5", "C4 M8 M10 A7", "B7 C6 C5 F9", "F11 A8 B8 G2", "M16 A10 B10 M9",
    "M11 M17 A16 B16", "M18 F12 F14 M19", "A9 B9 A11 B11", "M20 A17 B17 M12", "M14 A18 F13 F15", "A19 B18 B19 M21",
    "C7 C8 M13 M15", "A20 B20 M22 M23", "A12 A14 B12 B14", "C9 C10 C11 C16", "C17 C18 C19 A21", "B21 A13 B13 A15",
    "B15 G3 M24 M25", "A22 A23 B22 B23", "M26 M27 M28 M29", "M30 M31 D0 D1", "D2 D3 D4 D5", "D6 D7 D8 D9",
    "D10 D11 C12 D16", "A24 B24 C13 D17", "C14 A25 B25 C15", "D18 C20 C21 D19", "C22 C23 A26 B26", "A27 B27 A28 B28",
    "A29 B29 D12 A30", "B30 A31 B31 D13", "D14 D15 D20 D21", "D22 D23 C24 C25", "D24 C26 C27 D25", "C28 D26 C29 D27",
    "C30 D28 C31 D29", "D30 D31",
)
NX, NY = 4, 4
WINDOWS = (16, 8, 8)
PACE = 2


def parts(item):
    if item < EVENTS:
        return ((item, 0), (item, 1))
    first, second = PAIRS[(item - EVENTS) % 8]
    block = 2 + (item - EVENTS) // 8
    return ((first, block), (second, block))


def split(value):
    high = value.astype(BF16)
    low = (value - high.astype(F32)).astype(BF16)
    return high, low


def pick(table, index):
    value = jnp.int32(table[0])
    for place in range(1, len(table)):
        value = jnp.where(index == place, jnp.int32(table[place]), value)
    return value


def kernel(
    panel_hbm, ancestor_hbm, structure, diag_hbm, panel_out, diag_out,
    panel, ancestor, diag_inv, gathered, b_pair, b_high, b_low, a_high, a_low, own_high, own_low, partial, got1, got2, owned, got3, final, arrived, own_diag, got_diag,
    sum_diag, all_diag,
    gather_send, gather_recv, core_send, core_recv, pair_send, pair_recv, send1, recv1, send2, recv2, send3, recv3, send4, recv4,
    send5, recv5, send6, recv6, load_sem,
):
    row = lax.axis_index("prow")
    col = lax.axis_index("pcol")
    core = lax.rem(col, 2)
    zl = lax.rem(col // 2, 2)
    x = col // 4
    y = lax.rem(row, NY)
    zh = row // NY

    def at_col(xx, zz, cc):
        return (xx * 2 + zz) * 2 + cc

    right = (row, at_col(lax.rem(x + 1, NX), zl, core))
    left = (row, at_col(lax.rem(x + NX - 1, NX), zl, core))
    z_pair = (row, at_col(x, 1 - zl, core))
    twin = (row, at_col(x, zl, 1 - core))
    y_up, y_down, y_far = lax.rem(y + 1, NY), lax.rem(y + NY - 1, NY), lax.rem(y + 2, NY)
    up = (zh * NY + y_up, col)
    down = (zh * NY + y_down, col)
    z_far = ((1 - zh) * NY + y, col)
    home_rows = (x * 2 + zl, x * 2 + 1 - zl)

    barrier = pltpu.get_barrier_semaphore()

    def greet(device):
        pl.semaphore_signal(barrier, inc=1, device_id=device, device_id_type=MESH)

    greeted = (right, left, z_pair, twin, up, down, z_far)
    for device in greeted:
        greet(device)

    copies = [
        pltpu.make_async_copy(panel_hbm, panel, load_sem.at[0]),
        pltpu.make_async_copy(ancestor_hbm, ancestor, load_sem.at[1]),
        pltpu.make_async_copy(diag_hbm, diag_inv, load_sem.at[2]),
    ]
    for copy in copies:
        copy.start()
    for copy in copies:
        copy.wait()

    def take_columns(block, value):
        high, low = split(value)
        b_high[block] = high
        b_low[block] = low

    for block in range(2):
        take_columns(block, ancestor[:, block * 256 : (block + 1) * 256])

    def home_node(dx, unit):
        return at_col(lax.rem(x + NX + dx, NX), zl, core if unit == 0 else 1 - core)

    def load(event, unit, value):
        node = home_node(DX[event], unit)
        for block in range(4):
            mask = structure[node, row * 4 + block].astype(F32)
            high, low = split(value[:, block * 256 : (block + 1) * 256] * mask)
            a_high[event, unit * 64 : (unit + 1) * 64, block * 256 : (block + 1) * 256] = high
            a_low[event, unit * 64 : (unit + 1) * 64, block * 256 : (block + 1) * 256] = low

    for event in range(4):
        load(event, 0, panel[0, event * 64 : (event + 1) * 64, :])

    pl.semaphore_wait(barrier, len(greeted))

    sent = []

    def send(source, target, send_sem, recv_sem, device):
        copy = pltpu.make_async_remote_copy(
            src_ref=source, dst_ref=target, send_sem=send_sem, recv_sem=recv_sem, device_id=device, device_id_type=MESH
        )
        copy.start()
        sent.append(copy)

    def wait_recv(target, send_sem, recv_sem):
        pltpu.make_async_remote_copy(
            src_ref=target, dst_ref=target, send_sem=send_sem, recv_sem=recv_sem, device_id=twin, device_id_type=MESH
        ).wait_recv()

    def mine(event):
        if event < 4:
            return panel.at[0, pl.ds(event * 64, 64), :]
        return gathered.at[0, event]

    count = [0]

    def pass_on(event, table, device):
        if event in table:
            there = table[event]
            send(mine(event), gathered.at[0, there], gather_send.at[count[0]], gather_recv.at[there], device)
            count[0] += 1

    def to_twin(event):
        send(mine(event), gathered.at[1, event], core_send.at[event], core_recv.at[event], twin)

    def arrive(event):
        wait_recv(gathered.at[0, event], gather_send.at[0], gather_recv.at[event])
        pass_on(event, TO_RIGHT, right)
        pass_on(event, TO_LEFT, left)
        to_twin(event)

    def take_pair(block):
        wait_recv(b_pair.at[block - 2], pair_send.at[block - 2], pair_recv.at[block - 2])
        take_columns(block, b_pair[block - 2])

    def multiply(item):
        if item < EVENTS:
            if item >= 4:
                load(item, 0, mine(item))
            wait_recv(gathered.at[1, item], core_send.at[0], core_recv.at[item])
            load(item, 1, gathered.at[1, item])
        (event0, block0), (event1, block1) = parts(item)

        @pl.loop(0, 2)
        def _(n):
            event = event0 + n * (event1 - event0)
            block = block0 + n * (block1 - block0)
            high = a_high[event]
            product = (
                jnp.dot(high, b_high[block], preferred_element_type=F32)
                + jnp.dot(high, b_low[block], preferred_element_type=F32)
                + jnp.dot(a_low[event], b_high[block], preferred_element_type=F32)
            )
            for unit in range(2):
                for yy in range(NY):
                    start = unit * 64 + yy * 16
                    partial[item, yy, n, unit * 16 : (unit + 1) * 16, :] = product[start : start + 16, :]

        send(partial.at[item, y_far, 0], got1.at[item, 0], send1.at[item, 0], recv1.at[item, 0], up)
        send(partial.at[item, y_far, 1], got1.at[item, 1], send1.at[item, 1], recv1.at[item, 1], down)

    def stage2(item, way):
        yy, device = ((y_up, up), (y_down, down))[way]
        wait_recv(got1.at[item, way], send1.at[item, way], recv1.at[item, way])
        partial[item, yy, way] += got1[item, way]
        send(partial.at[item, yy], got2.at[item, way], send2.at[item, way], recv2.at[item, way], device)

    def stage3(item):
        for way in range(2):
            wait_recv(got2.at[item, way], send2.at[item, way], recv2.at[item, way])
        for n in range(2):
            total = partial[item, y, n] + got2[item, 0, n] + got2[item, 1, n]
            for unit in range(2):
                for hz in range(2):
                    start = unit * 16 + hz * 8
                    owned[item, hz, unit, n] = total[start : start + 8, :]
        send(owned.at[item, 1 - zh], got3.at[item], send3.at[item], recv3.at[item], z_far)

    def stage4(item):
        wait_recv(got3.at[item], send3.at[item], recv3.at[item])
        final[item] = owned[item, zh] + got3[item]

    def send_piece(item, dx, own, place, unit, act):
        node = home_node(dx, unit)
        home_row = home_rows[0] if own else home_rows[1]
        here = jnp.logical_and(home_row == row, node == col)
        rows = pl.ds(pl.multiple_of(y * 16 + zh * 8, 8), 8)
        if own:
            target = arrived.at[core, :, place, rows, :]
        else:
            quarters = pl.ds(lax.rem(place, 2) * 2, 2)
            target = arrived.at[core, place // 2, quarters, rows, :]
        copy = pltpu.make_async_remote_copy(
            src_ref=final.at[item, unit], dst_ref=target, send_sem=send4.at[item, unit], recv_sem=recv4.at[core, place, row],
            device_id=(home_row, node), device_id_type=MESH,
        )
        if act:

            @pl.when(here)
            def _():
                if own:
                    arrived[core, :, place, rows, :] = final[item, unit]
                else:
                    arrived[core, place // 2, quarters, rows, :] = final[item, unit]

        @pl.when(jnp.logical_not(here))
        def _():
            if act:
                copy.start()
            else:
                copy.wait_send()

    ITEM_DX = DX + tuple(DX[parts(item)[0][0]] for item in range(EVENTS, ITEMS))
    ITEM_PLACE = QUARTER + tuple(
        (parts(item)[0][1] - 2) * 2 + QUARTER[parts(item)[0][0]] // 2 for item in range(EVENTS, ITEMS)
    )

    def send_home(items, turn):
        item = pick(items, lax.rem(row + turn, len(items)))
        dx = pick(ITEM_DX, item)
        place = pick(ITEM_PLACE, item)
        for unit in range(2):

            @pl.when(item < EVENTS)
            def _():
                send_piece(item, dx, True, place, unit, True)

            @pl.when(item >= EVENTS)
            def _():
                send_piece(item, dx, False, place, unit, True)

    for turn in range(2):
        pass_on(turn, TO_RIGHT, right)
        pass_on(3 - turn, TO_LEFT, left)
    for block in range(2):
        send(ancestor.at[:, pl.ds(block * 256, 256)], b_pair.at[block], pair_send.at[block], pair_recv.at[block], z_pair)
    for event in range(4):
        to_twin(event)
    for turn in range(2, 4):
        pass_on(turn, TO_RIGHT, right)
        pass_on(3 - turn, TO_LEFT, left)
    work = {
        "F": arrive,
        "G": take_pair,
        "M": multiply,
        "A": lambda item: stage2(item, 0),
        "B": lambda item: stage2(item, 1),
        "C": stage3,
        "D": stage4,
    }
    batch, ready, sizes = [], [], list(WINDOWS)
    for step in " ".join(ORDER).split():
        item = int(step[1:])
        work[step[0]](item)
        if step[0] == "D":
            batch.append(item)
            for _ in range(min(PACE, len(ready))):
                send_home(*ready.pop(0))
            if len(batch) == sizes[0]:
                ready += [(tuple(batch), turn) for turn in range(len(batch))]
                batch = []
                sizes.pop(0)
    for items, turn in ready:
        send_home(items, turn)

    for block in range(4):
        mask = structure[col, row * 4 + block].astype(F32)
        high, low = split(panel[0, :, block * 256 : (block + 1) * 256] * mask)
        own_high[:, block * 256 : (block + 1) * 256] = high
        own_low[:, block * 256 : (block + 1) * 256] = low

    contract = functools.partial(
        lax.dot_general, dimension_numbers=(((1,), (1,)), ((), ())), preferred_element_type=F32
    )
    from_own = lax.rem(row, 2) == zl

    def take(side, place):
        for source in range(8):
            there = jnp.logical_and(source == row, at_col(row // 2, zl, side) == col)

            @pl.when(jnp.logical_not(there))
            def _():
                wait_recv(final.at[0, 0], send4.at[0, 0], recv4.at[side, place, source])

    total = jnp.zeros((256, 256), F32)
    for block in range(2):
        for side in range(2):
            for half in range(2):
                take_now = (block * 2 + half,)

                @pl.when(jnp.logical_not(from_own))
                def _():
                    take(side, take_now[0])

            if block == 0:

                @pl.when(from_own)
                def _():
                    for place in range(4):
                        take(side, place)

            columns = slice(side * 512 + block * 256, side * 512 + block * 256 + 256)
            value = arrived[side, block].reshape(256, 256)
            panel_out[:, columns] = value
            high, low = split(value)
            right_high = own_high[:, columns]
            right_low = own_low[:, columns]
            total = total + contract(high, right_high) + contract(high, right_low) + contract(low, right_high)
    own_diag[...] = total
    for step in range(1, 8):
        other = lax.rem(row + step, 8)
        piece = pl.ds(pl.multiple_of(other * 32, 32), 32)
        send(own_diag.at[piece, :], got_diag.at[row], send5.at[step], recv5.at[row], (other, col))
    for copy in sent[:-7]:
        copy.wait_send()
    here = pl.ds(pl.multiple_of(row * 32, 32), 32)
    result = diag_inv[0, here, :] + own_diag[here, :]
    for step in range(1, 8):
        other = lax.rem(row + step, 8)
        wait_recv(got_diag.at[other], send5.at[step], recv5.at[other])
        result = result + got_diag[other]
    sum_diag[...] = result
    for step in range(1, 8):
        other = lax.rem(row + step, 8)
        send(sum_diag, all_diag.at[row], send6.at[step], recv6.at[row], (other, col))
    diag_out[0, here, :] = result
    for item in range(ITEMS):
        for unit in range(2):
            send_piece(item, ITEM_DX[item], item < EVENTS, ITEM_PLACE[item], unit, False)
    for step in range(1, 8):
        other = lax.rem(row + step, 8)
        wait_recv(all_diag.at[other], send6.at[step], recv6.at[other])
        diag_out[0, pl.ds(pl.multiple_of(other * 32, 32), 32), :] = all_diag[other]

    for copy in sent[-14:]:
        copy.wait_send()


def local(panel_t, ancestor, structure, diag_inv):
    vmem = pltpu.VMEM
    dma = pltpu.SemaphoreType.DMA
    product, diag = pl.pallas_call(
        kernel,
        out_shape=(
            vmem((256, 1024), F32),
            vmem((1, 256, 256), F32),
        ),
        in_specs=[
            pl.BlockSpec(memory_space=pl.ANY),
            pl.BlockSpec(memory_space=pl.ANY),
            pl.BlockSpec(memory_space=pltpu.SMEM),
            pl.BlockSpec(memory_space=pl.ANY),
        ],
        out_specs=(pl.BlockSpec(memory_space=vmem), pl.BlockSpec(memory_space=vmem)),
        scratch_shapes=[
            vmem((1, 256, 1024), F32),
            vmem((1024, 512), F32),
            vmem((1, 256, 256), F32),
            vmem((2, EVENTS, 64, 1024), F32),
            vmem((2, 1024, 256), F32),
            vmem((4, 1024, 256), BF16),
            vmem((4, 1024, 256), BF16),
            vmem((EVENTS, 128, 1024), BF16),
            vmem((EVENTS, 128, 1024), BF16),
            vmem((256, 1024), BF16),
            vmem((256, 1024), BF16),
            vmem((ITEMS, NY, 2, 32, 256), F32),
            vmem((ITEMS, 2, 32, 256), F32),
            vmem((ITEMS, 2, 2, 32, 256), F32),
            vmem((ITEMS, 2, 2, 2, 8, 256), F32),
            vmem((ITEMS, 2, 2, 8, 256), F32),
            vmem((ITEMS, 2, 2, 8, 256), F32),
            vmem((2, 2, 4, 64, 256), F32),
            vmem((256, 256), F32),
            vmem((8, 32, 256), F32),
            vmem((32, 256), F32),
            vmem((8, 32, 256), F32),
            dma((12,)),
            dma((EVENTS,)),
            dma((EVENTS,)),
            dma((EVENTS,)),
            dma((2,)),
            dma((2,)),
            dma((ITEMS, 2)),
            dma((ITEMS, 2)),
            dma((ITEMS, 2)),
            dma((ITEMS, 2)),
            dma((ITEMS,)),
            dma((ITEMS,)),
            dma((ITEMS, 2)),
            dma((2, 4, 8)),
            dma((8,)),
            dma((8,)),
            dma((8,)),
            dma((8,)),
            dma((3,)),
        ],
        compiler_params=pltpu.CompilerParams(
            collective_id=0, has_side_effects=True, vmem_limit_bytes=60 * 1024 * 1024
        ),
        name="level_update",
    )(panel_t, ancestor, structure, diag_inv)
    return -product, diag


def solution(mesh):
    return jax.shard_map(
        local,
        mesh=mesh,
        in_specs=(P("pcol", None, "prow"), P("prow", "pcol"), P(), P("pcol", None, None)),
        out_specs=(P("pcol", "prow"), P("pcol", None, None)),
        check_vma=False,
    )
```

time: 133 us -> 125 us (0.940)
  Pallas kernels: 129 us -> 122 us
  local copies, waits for them, and re-layouts: 3.06 us -> 0.7 us
    pallas_call x1, Pallas kernels: 129 us -> 122 us  [local(): pl.pallas_call(kernel, out_shape=(vmem((256, 1024), F32), vmem((1, 256, 2...]
    unnamed x4 -> x1, local copies, waits for them, and re-layouts: 3.06 us -> 0.7 us
where the time goes in v3:
time: 125 us
  Pallas kernels  122 us (98%)
    pallas_call x1, Pallas kernels, local(): pl.pallas_call(kernel, out_shape=(vmem((256, 1024), F32), vmem((1, 256, 2...  122 us

profile of v3, /device:TPU:32, one launch (start us, length us, event | category | flops | bytes accessed | tf_op | source)
XLA Modules:
  0.0 124.9 jit_solution(16736983327940274126)
XLA Ops:
  0.6 122.5 %level_update.1 = (f32[256,1024]{1,0:T(8,128)S(1)}, f32[1,256,256]{2,1,0:T(8,128)S(1)}) custom-call(f32[1,256,1024]{2,1,0:T(8,128)} %panel_hbm.1, f32[1024,512]{1,0:T(8,128)} %ancestor_hbm.1, s32[16,32]{1,0:T(8,128)} %structure.1, f32[1,256,256]{2,1,0:T(8,128)} %diag_hbm.1), custom_call_target="tpu_custom_call" | custom-call | tf_op jit(solution)/shard_map/level_update/pallas_call | solution.py:374
  123.1 1.1 neg.3
  124.2 0.7 copy.7

commit v4 on v3

--- a/solution.py
+++ b/solution.py
@@ -29,8 +29,6 @@
     "C30 D28 C31 D29", "D30 D31",
 )
 NX, NY = 4, 4
-WINDOWS = (16, 8, 8)
-PACE = 2
 
 
 def parts(item):
@@ -246,6 +244,12 @@
     ITEM_PLACE = QUARTER + tuple(
         (parts(item)[0][1] - 2) * 2 + QUARTER[parts(item)[0][0]] // 2 for item in range(EVENTS, ITEMS)
     )
+
+    def spread(chips):
+        order, lists = [], [list(items) for items in chips.values()]
+        while any(lists):
+            order += [items.pop(0) for items in lists if items]
+        return tuple(order)
 
     def send_home(items, turn):
         item = pick(items, lax.rem(row + turn, len(items)))
@@ -280,20 +284,14 @@
         "C": stage3,
         "D": stage4,
     }
-    batch, ready, sizes = [], [], list(WINDOWS)
     for step in " ".join(ORDER).split():
-        item = int(step[1:])
-        work[step[0]](item)
-        if step[0] == "D":
-            batch.append(item)
-            for _ in range(min(PACE, len(ready))):
-                send_home(*ready.pop(0))
-            if len(batch) == sizes[0]:
-                ready += [(tuple(batch), turn) for turn in range(len(batch))]
-                batch = []
-                sizes.pop(0)
-    for items, turn in ready:
-        send_home(items, turn)
+        work[step[0]](int(step[1:]))
+    chips = {}
+    for item in range(ITEMS):
+        chips.setdefault((ITEM_DX[item], item < EVENTS), []).append(item)
+    turns = spread(chips)
+    for turn in range(ITEMS):
+        send_home(turns, turn)
 
     for block in range(4):
         mask = structure[col, row * 4 + block].astype(F32)

time: 125 us -> 123 us (0.984)
  Pallas kernels: 122 us -> 119 us
    pallas_call x1, Pallas kernels: 122 us -> 119 us  [local(): pl.pallas_call(kernel, out_shape=(vmem((256, 1024), F32), vmem((1, 256, 2...]
where the time goes in v4:
time: 123 us; the launch traced here: 122 us
  Pallas kernels  119 us (97%)
    pallas_call x1, Pallas kernels, local(): pl.pallas_call(kernel, out_shape=(vmem((256, 1024), F32), vmem((1, 256, 2...  119 us

profile of v4, /device:TPU:32, one launch (start us, length us, event | category | flops | bytes accessed | tf_op | source)
XLA Modules:
  0.0 121.7 jit_solution(9144060602612162206)
XLA Ops:
  0.6 119.3 %level_update.1 = (f32[256,1024]{1,0:T(8,128)S(1)}, f32[1,256,256]{2,1,0:T(8,128)S(1)}) custom-call(f32[1,256,1024]{2,1,0:T(8,128)} %panel_hbm.1, f32[1024,512]{1,0:T(8,128)} %ancestor_hbm.1, s32[16,32]{1,0:T(8,128)} %structure.1, f32[1,256,256]{2,1,0:T(8,128)} %diag_hbm.1), custom_call_target="tpu_custom_call" | custom-call | tf_op jit(solution)/shard_map/level_update/pallas_call | solution.py:372
  119.9 1.1 neg.3
  121.0 0.7 copy.7

commit v5 on v4

--- a/solution.py
+++ b/solution.py
@@ -20,13 +20,13 @@
 ITEMS = 32
 ORDER = (
     "M0 M1 M2 M3", "A0 B0 A1 B1", "F4 F6 A2 B2", "A3 B3 M4 M6", "C0 C1 F5 F7", "C2 C3 M5 A4",
-    "A6 B4 B6 M7", "F8 F10 A5 B5", "C4 M8 M10 A7", "B7 C6 C5 F9", "F11 A8 B8 G2", "M16 A10 B10 M9",
-    "M11 M17 A16 B16", "M18 F12 F14 M19", "A9 B9 A11 B11", "M20 A17 B17 M12", "M14 A18 F13 F15", "A19 B18 B19 M21",
-    "C7 C8 M13 M15", "A20 B20 M22 M23", "A12 A14 B12 B14", "C9 C10 C11 C16", "C17 C18 C19 A21", "B21 A13 B13 A15",
-    "B15 G3 M24 M25", "A22 A23 B22 B23", "M26 M27 M28 M29", "M30 M31 D0 D1", "D2 D3 D4 D5", "D6 D7 D8 D9",
-    "D10 D11 C12 D16", "A24 B24 C13 D17", "C14 A25 B25 C15", "D18 C20 C21 D19", "C22 C23 A26 B26", "A27 B27 A28 B28",
-    "A29 B29 D12 A30", "B30 A31 B31 D13", "D14 D15 D20 D21", "D22 D23 C24 C25", "D24 C26 C27 D25", "C28 D26 C29 D27",
-    "C30 D28 C31 D29", "D30 D31",
+    "A6 B4 B6 M7", "F8 F10 A5 B5", "M8 M10 C4 C6", "A7 B7 F9 F11", "G2 M16 A8 B8", "M17 A10 B10 M9",
+    "M11 A16 B16 M18", "F12 F14 M19 A17", "B17 M20 M12 A9", "B9 M14 A11 B11", "F13 F15 M21 C5", "A18 B18 C7 C8",
+    "A19 B19 C10 M13", "M15 A12 A20 B12", "B20 M22 M23 A14", "B14 C9 C16 C17", "C11 A21 B21 C18", "G3 M24 A13 A15",
+    "B13 B15 M25 M26", "M27 M28 A22 B22", "A23 B23 M29 M30", "M31 C12 C14 C19", "A24 B24 C20 C21", "D0 D1 D2 D3",
+    "D4 D5 C13 D6", "D7 D8 D9 D10", "D11 D16 D17 D18", "C15 A25 B25 D12", "A26 B26 D14 A27", "B27 D19 A28 B28",
+    "D20 D21 C22 D13", "D15 C23 A29 B29", "A30 B30 A31 B31", "D22 C24 D23 C25", "C26 C27 D24 C28", "D25 C29 D26 C30",
+    "D27 C31 D28 D29", "D30 D31",
 )
 NX, NY = 4, 4
 

time: 123 us -> 123 us (level)
  no operation moved by 1% of the time
where the time goes in v5:
time: 123 us; the launch traced here: 121 us
  Pallas kernels  119 us (97%)
    pallas_call x1, Pallas kernels, local(): pl.pallas_call(kernel, out_shape=(vmem((256, 1024), F32), vmem((1, 256, 2...  119 us

profile of v5, /device:TPU:32, one launch (start us, length us, event | category | flops | bytes accessed | tf_op | source)
XLA Modules:
  0.0 121.3 jit_solution(7503169444925173530)
XLA Ops:
  0.6 118.9 %level_update.1 = (f32[256,1024]{1,0:T(8,128)S(1)}, f32[1,256,256]{2,1,0:T(8,128)S(1)}) custom-call(f32[1,256,1024]{2,1,0:T(8,128)} %panel_hbm.1, f32[1024,512]{1,0:T(8,128)} %ancestor_hbm.1, s32[16,32]{1,0:T(8,128)} %structure.1, f32[1,256,256]{2,1,0:T(8,128)} %diag_hbm.1), custom_call_target="tpu_custom_call" | custom-call | tf_op jit(solution)/shard_map/level_update/pallas_call | solution.py:372
  119.5 1.1 neg.3
  120.6 0.7 copy.7
